TPU v7x, 32 devices: a whole 2x2x4 slice. The times are simulated.
32 devices in a mesh: rows: 8 (over z, y), cols: 4 (over x, core).
Axes of the slice: x: 2, y: 2, z: 4, core: 2. Of those that a mesh axis runs over, the one named last changes fastest.
Arguments:
- adjacency_tiles: bfloat16 [192, 12, 128, 128], P(('rows', 'cols')), may hold values from 2.170139e-08 to 0.25
- col_block: int32 [192, 12], P(('rows', 'cols')), may hold values from 0 to 191, as said below
- label_prior: float32 [24576, 256], P(('rows', 'cols')), may hold values from 0.05 to 20.1
- seed_label: int32 [24576], P(('rows', 'cols')), may hold values from 0 to 255
- seed_mask: int32 [24576], P(('rows', 'cols')), may hold values 0 or 1
Outputs:
- labels: float32 [24576, 256], P(('rows', 'cols'))
Inputs may be any that keep to these rules, and one draw needn't show every extreme that they name: Row block b is held by device b // 6 of rows+cols, whose rows group is b // (6 * 4). col_block[b, 0] = b. For each device, all its tiles that reference blocks of another rows group reference one and the same block of that group, and each device references every rows group.
All inputs are finite; a program needn't handle non-finite values. No bound on the sum of `seed_mask` on one device may be relied on, other than what follows from the above.
Results may differ from a plain program's by a relative error of at most 0.00041.
Values may be sent and summed in bfloat16 or wider, within the bound.
A program may use at most 64 MiB of HBM per device.

v0:
```python
import jax
import jax.numpy as jnp
from jax import lax
from jax.sharding import PartitionSpec as P

HOPS = 4
ALPHA = 0.85
SEED_BOOST = 8.0


def prepare(label_prior, seed_label, seed_mask):
    classes = label_prior.shape[1]
    one_hot = (seed_label[:, None] == jnp.arange(classes, dtype=jnp.int32)[None, :]).astype(
        jnp.float32
    )
    anchor_raw = label_prior + SEED_BOOST * seed_mask[:, None].astype(jnp.float32) * one_hot
    return anchor_raw * (classes / jnp.sum(anchor_raw, axis=1, keepdims=True))


def ask_blocks(owner_group, within, own_group, n_rows):
    group_ids = jnp.arange(n_rows, dtype=jnp.int32)
    matched = owner_group.reshape(-1)[:, None] == group_ids[None, :]
    wanted = jnp.max(jnp.where(matched, within.reshape(-1)[:, None], 0), axis=0)
    wanted = jnp.where(group_ids == own_group, 0, wanted)
    return lax.all_to_all(
        wanted.reshape(n_rows, 1), "rows", split_axis=0, concat_axis=0, tiled=True
    )


def local(adjacency_tiles, col_block, label_prior, seed_label, seed_mask):
    blocks_dev = adjacency_tiles.shape[0]
    degree = adjacency_tiles.shape[1]
    block_rows = adjacency_tiles.shape[2]
    classes = label_prior.shape[1]
    n_rows = lax.axis_size("rows")
    n_cols = lax.axis_size("cols")
    group_size = n_cols * blocks_dev
    own_group = lax.axis_index("rows")
    owner_group = col_block // group_size
    within = col_block % group_size
    table_index = jnp.where(owner_group == own_group, within, group_size + owner_group).reshape(-1)
    anchor = prepare(label_prior, seed_label, seed_mask)
    labels = anchor
    for hop_index in range(HOPS):
        asked = ask_blocks(owner_group, within, own_group, n_rows)
        sent_blocks = labels.astype(jnp.bfloat16).reshape(blocks_dev, block_rows, classes)
        group_blocks = lax.all_gather(sent_blocks, "cols", axis=0, tiled=True)
        reply = group_blocks[asked[:, 0]]
        remote = lax.all_to_all(reply, "rows", split_axis=0, concat_axis=0, tiled=True)
        table = jnp.concatenate([group_blocks, remote], axis=0)
        operand = table[table_index].reshape(blocks_dev, degree, block_rows, classes)
        spread = jnp.einsum(
            "bkij,bkjc->bic", adjacency_tiles, operand, preferred_element_type=jnp.float32
        )
        spread = spread.reshape(blocks_dev * block_rows, classes)
        blended = ALPHA * spread + (1.0 - ALPHA) * anchor
        labels = blended * (classes / jnp.sum(blended, axis=1, keepdims=True))
    return labels


def solution(mesh):
    in_specs = (
        P(("rows", "cols"), None, None, None),
        P(("rows", "cols"), None),
        P(("rows", "cols"), None),
        P(("rows", "cols")),
        P(("rows", "cols")),
    )
    out_specs = P(("rows", "cols"), None)
    return jax.shard_map(local, mesh=mesh, in_specs=in_specs, out_specs=out_specs, check_vma=False)
```

profile of v0, /device:TPU:0, one launch (start us, length us, event | category | flops | bytes accessed | tf_op | source)
XLA Modules:
  0.0 247.3 jit_solution(12359041004204754055)
XLA Ops:
  6.5 0.9 convert_multiply_fusion
  7.4 1.5 fusion.11
  8.9 2.3 multiply_convert_fusion.3
  11.3 0.1 eq.37
  11.3 0.1 broadcast_in_dim.56
  11.4 0.1 select_reduce_fusion
  11.5 0.1 copy.8
  11.6 13.6 %all_to_all.32 = s32[8,1,1]{2,1,0:T(1,128)S(1)} all-to-all(s32[8,1,1]{2,1,0:T(1,128)S(1)} %copy.8), channel_id=1, replica_groups=mesh['rows'=8,'cols'=4] {'rows'}, dimensions={0} | all-to-all | bytes 64 | tf_op jit(solution)/shard_map/all_to_all | solution.py:25
  25.2 0.2 reduce
  25.5 8.3 %all-gather.5.cloned.1.call-done = bf16[24,128,256]{2,1,0:T(8,128)(2,1)} async-done(((bf16[6,128,256]{2,1,0:T(8,128)(2,1)}), bf16[24,128,256]{2,1,0:T(8,128)(2,1)}) %all-gather.5.cloned.1.call-update) | async-done | bytes 1572880 | tf_op jit(solution)/shard_map/all_gather | solution.py:47
  33.7 2.8 %gather_fusion = bf16[8,128,256]{2,1,0:T(8,128)(2,1)} fusion(bf16[24,128,256]{2,1,0:T(8,128)(2,1)} %all-gather.5.cloned.1.call-done, s32[1024]{0:T(1024)S(1)} %pad_clamp_fusion.1), kind=kCustom, calls=%fused_computation | custom fusion | bytes 1048608 | tf_op jit(solution)/shard_map/gather | solution.py:48
  36.5 5.5 %all-to-all-start.1 = ((bf16[8,128,256]{2,1,0:T(8,128)(2,1)}), bf16[8,128,256]{2,1,0:T(8,128)(2,1)S(1)}, u32[]{:S(2)}, u32[]{:S(2)}) async-start(bf16[8,128,256]{2,1,0:T(8,128)(2,1)} %gather_fusion), calls=%async_computation.1 | async-start | bytes 1048576 | tf_op jit(solution)/shard_map/all_to_all | solution.py:49
  42.0 0.0 all-gather.7.cloned.1.call-start
  42.1 0.1 reshape.143
  42.2 14.7 %all-to-all-done.1 = bf16[8,128,256]{2,1,0:T(8,128)(2,1)S(1)} async-done(((bf16[8,128,256]{2,1,0:T(8,128)(2,1)}), bf16[8,128,256]{2,1,0:T(8,128)(2,1)S(1)}, u32[]{:S(2)}, u32[]{:S(2)}) %all-to-all-start.1) | async-done | bytes 524320 | tf_op jit(solution)/shard_map/all_to_all | solution.py:49
  56.9 3.0 %pad_maximum_fusion = bf16[32,128,256]{2,1,0:T(8,128)(2,1)} fusion(bf16[8,128,256]{2,1,0:T(8,128)(2,1)S(1)} %all-to-all-done.1, bf16[24,128,256]{2,1,0:T(8,128)(2,1)} %all-gather.5.cloned.1.call-done), kind=kLoop, calls=%fused_computation.8 | loop fusion | flops 1048576 | bytes 4194304 | tf_op jit(solution)/shard_map/concatenate | solution.py:50
  59.9 7.0 %gather_fusion.1 = bf16[72,128,256]{2,1,0:T(8,128)(2,1)} fusion(bf16[32,128,256]{2,1,0:T(8,128)(2,1)} %pad_maximum_fusion, s32[1024]{0:T(1024)S(1)} %pad_clamp_fusion), kind=kCustom, calls=%fused_computation.1 | custom fusion | bytes 9437472 | tf_op jit(solution)/shard_map/gather | solution.py:51
  66.9 3.3 %fusion = f32[6,256,128]{1,2,0:T(8,128)S(1)} fusion(bf16[6,12,128,128]{3,2,1,0:T(8,128)(2,1)S(1)} %copy-done, bf16[6,12,128,256]{3,2,1,0:T(8,128)(2,1)} %bitcast.77), kind=kOutput, calls=%fused_computation.16 | convolution fusion | flops 604176384 | bytes 7864320 | tf_op jit(solution)/shard_map/bkij,bkjc->bic/dot_general | solution.py:52
  70.3 0.5 fusion.4
  70.8 1.3 multiply_convert_fusion.2
  72.1 0.0 all-gather.7.cloned.1.call-update
  72.1 0.0 all-gather.9.cloned.1.call-start
  72.1 17.9 %all-gather.7.cloned.1.call-done = bf16[24,128,256]{2,1,0:T(8,128)(2,1)} async-done(((bf16[6,128,256]{2,1,0:T(8,128)(2,1)}), bf16[24,128,256]{2,1,0:T(8,128)(2,1)}) %all-gather.7.cloned.1.call-update) | async-done | bytes 1572880 | tf_op jit(solution)/shard_map/all_gather | solution.py:47
  90.0 2.8 %gather_fusion.2 = bf16[8,128,256]{2,1,0:T(8,128)(2,1)} fusion(bf16[24,128,256]{2,1,0:T(8,128)(2,1)} %all-gather.7.cloned.1.call-done, s32[1024]{0:T(1024)S(1)} %pad_clamp_fusion.1), kind=kCustom, calls=%fused_computation.2 | custom fusion | bytes 1048608 | tf_op jit(solution)/shard_map/gather | solution.py:48
  92.8 20.4 %all_to_all.33 = bf16[8,128,256]{2,1,0:T(8,128)(2,1)S(1)} all-to-all(bf16[8,128,256]{2,1,0:T(8,128)(2,1)} %gather_fusion.2), channel_id=1, replica_groups=mesh['rows'=8,'cols'=4] {'rows'}, dimensions={0} | all-to-all | bytes 1048576 | tf_op jit(solution)/shard_map/all_to_all | solution.py:49
  113.2 3.0 %pad_maximum_fusion.1 = bf16[32,128,256]{2,1,0:T(8,128)(2,1)} fusion(bf16[8,128,256]{2,1,0:T(8,128)(2,1)S(1)} %all_to_all.33, bf16[24,128,256]{2,1,0:T(8,128)(2,1)} %all-gather.7.cloned.1.call-done), kind=kLoop, calls=%fused_computation.9 | loop fusion | flops 1048576 | bytes 4194304 | tf_op jit(solution)/shard_map/concatenate | solution.py:50
  116.1 7.0 %gather_fusion.3 = bf16[72,128,256]{2,1,0:T(8,128)(2,1)} fusion(bf16[32,128,256]{2,1,0:T(8,128)(2,1)} %pad_maximum_fusion.1, s32[1024]{0:T(1024)S(1)} %pad_clamp_fusion), kind=kCustom, calls=%fused_computation.3 | custom fusion | bytes 9437472 | tf_op jit(solution)/shard_map/gather | solution.py:51
  123.2 3.2 %fusion.1 = f32[6,256,128]{1,2,0:T(8,128)S(1)} fusion(bf16[6,12,128,128]{3,2,1,0:T(8,128)(2,1)S(1)} %copy-done, bf16[6,12,128,256]{3,2,1,0:T(8,128)(2,1)} %bitcast.78), kind=kOutput, calls=%fused_computation.17 | convolution fusion | flops 604176384 | bytes 7864320 | tf_op jit(solution)/shard_map/bkij,bkjc->bic/dot_general | solution.py:52
  126.4 0.5 fusion.5
  127.0 1.3 multiply_convert_fusion.1
  128.2 0.0 all-gather.9.cloned.1.call-update
  128.3 0.0 all-gather.11.cloned.1.call-start
  128.3 17.9 %all-gather.9.cloned.1.call-done = bf16[24,128,256]{2,1,0:T(8,128)(2,1)} async-done(((bf16[6,128,256]{2,1,0:T(8,128)(2,1)}), bf16[24,128,256]{2,1,0:T(8,128)(2,1)}) %all-gather.9.cloned.1.call-update) | async-done | bytes 1572880 | tf_op jit(solution)/shard_map/all_gather | solution.py:47
  146.2 2.8 %gather_fusion.4 = bf16[8,128,256]{2,1,0:T(8,128)(2,1)} fusion(bf16[24,128,256]{2,1,0:T(8,128)(2,1)} %all-gather.9.cloned.1.call-done, s32[1024]{0:T(1024)S(1)} %pad_clamp_fusion.1), kind=kCustom, calls=%fused_computation.4 | custom fusion | bytes 1048608 | tf_op jit(solution)/shard_map/gather | solution.py:48
  149.0 20.4 %all_to_all.34 = bf16[8,128,256]{2,1,0:T(8,128)(2,1)S(1)} all-to-all(bf16[8,128,256]{2,1,0:T(8,128)(2,1)} %gather_fusion.4), channel_id=1, replica_groups=mesh['rows'=8,'cols'=4] {'rows'}, dimensions={0} | all-to-all | bytes 1048576 | tf_op jit(solution)/shard_map/all_to_all | solution.py:49
  169.4 3.0 %pad_maximum_fusion.2 = bf16[32,128,256]{2,1,0:T(8,128)(2,1)} fusion(bf16[8,128,256]{2,1,0:T(8,128)(2,1)S(1)} %all_to_all.34, bf16[24,128,256]{2,1,0:T(8,128)(2,1)} %all-gather.9.cloned.1.call-done), kind=kLoop, calls=%fused_computation.10 | loop fusion | flops 1048576 | bytes 4194304 | tf_op jit(solution)/shard_map/concatenate | solution.py:50
  172.3 7.0 %gather_fusion.5 = bf16[72,128,256]{2,1,0:T(8,128)(2,1)} fusion(bf16[32,128,256]{2,1,0:T(8,128)(2,1)} %pad_maximum_fusion.2, s32[1024]{0:T(1024)S(1)} %pad_clamp_fusion), kind=kCustom, calls=%fused_computation.5 | custom fusion | bytes 9437472 | tf_op jit(solution)/shard_map/gather | solution.py:51
  179.4 3.2 %fusion.2 = f32[6,256,128]{1,2,0:T(8,128)S(1)} fusion(bf16[6,12,128,128]{3,2,1,0:T(8,128)(2,1)S(1)} %copy-done, bf16[6,12,128,256]{3,2,1,0:T(8,128)(2,1)} %bitcast.79), kind=kOutput, calls=%fused_computation.18 | convolution fusion | flops 604176384 | bytes 7864320 | tf_op jit(solution)/shard_map/bkij,bkjc->bic/dot_general | solution.py:52
  182.6 0.5 fusion.6
  183.2 1.3 multiply_convert_fusion
  184.5 17.9 %all-gather.11.cloned.1.call-done = bf16[24,128,256]{2,1,0:T(8,128)(2,1)} async-done(((bf16[6,128,256]{2,1,0:T(8,128)(2,1)}), bf16[24,128,256]{2,1,0:T(8,128)(2,1)}) %all-gather.11.cloned.1.call-update) | async-done | bytes 1572880 | tf_op jit(solution)/shard_map/all_gather | solution.py:47
  202.4 2.8 %gather_fusion.6 = bf16[8,128,256]{2,1,0:T(8,128)(2,1)} fusion(bf16[24,128,256]{2,1,0:T(8,128)(2,1)} %all-gather.11.cloned.1.call-done, s32[1024]{0:T(1024)S(1)} %pad_clamp_fusion.1), kind=kCustom, calls=%fused_computation.6 | custom fusion | bytes 1048608 | tf_op jit(solution)/shard_map/gather | solution.py:48
  205.2 20.4 %all_to_all.35 = bf16[8,128,256]{2,1,0:T(8,128)(2,1)S(1)} all-to-all(bf16[8,128,256]{2,1,0:T(8,128)(2,1)} %gather_fusion.6), channel_id=1, replica_groups=mesh['rows'=8,'cols'=4] {'rows'}, dimensions={0} | all-to-all | bytes 1048576 | tf_op jit(solution)/shard_map/all_to_all | solution.py:49
  225.6 3.0 %pad_maximum_fusion.3 = bf16[32,128,256]{2,1,0:T(8,128)(2,1)} fusion(bf16[8,128,256]{2,1,0:T(8,128)(2,1)S(1)} %all_to_all.35, bf16[24,128,256]{2,1,0:T(8,128)(2,1)} %all-gather.11.cloned.1.call-done), kind=kLoop, calls=%fused_computation.11 | loop fusion | flops 1048576 | bytes 4194304 | tf_op jit(solution)/shard_map/concatenate | solution.py:50
  228.5 7.0 %gather_fusion.7 = bf16[72,128,256]{2,1,0:T(8,128)(2,1)} fusion(bf16[32,128,256]{2,1,0:T(8,128)(2,1)} %pad_maximum_fusion.3, s32[1024]{0:T(1024)S(1)} %pad_clamp_fusion), kind=kCustom, calls=%fused_computation.7 | custom fusion | bytes 9437472 | tf_op jit(solution)/shard_map/gather | solution.py:51
  235.6 3.2 %fusion.3 = f32[6,256,128]{1,2,0:T(8,128)S(1)} fusion(bf16[6,12,128,128]{3,2,1,0:T(8,128)(2,1)S(1)} %copy-done, bf16[6,12,128,256]{3,2,1,0:T(8,128)(2,1)} %bitcast.76), kind=kOutput, calls=%fused_computation.19 | convolution fusion | flops 604176384 | bytes 7864320 | tf_op jit(solution)/shard_map/bkij,bkjc->bic/dot_general | solution.py:52
  238.8 0.5 fusion.7
  239.3 1.4 broadcast_multiply_fusion
  (22 shorter events, 0.1 us)
Async XLA Ops:
  6.5 60.4 %copy-start = (bf16[6,12,128,128]{3,2,1,0:T(8,128)(2,1)S(1)}, bf16[6,12,128,128]{3,2,1,0:T(8,128)(2,1)}, u32[]{:S(2)}) copy-start(bf16[6,12,128,128]{3,2,1,0:T(8,128)(2,1)} %param.5) | copy-start | bytes 7077892
  6.5 4.7 %copy-start.3 = (s32[6,12]{1,0:T(8,128)S(1)}, s32[6,12]{1,0:T(8,128)}, u32[]{:S(2)}) copy-start(s32[6,12]{1,0:T(8,128)} %param.6) | copy-start | bytes 868
  6.5 27.2 %all-gather.5.cloned.1.call-start = ((), (), s32[]{:S(2)}) async-start(), calls=%async_computation.5 | async-start | bytes 1966080 | tf_op jit(solution)/shard_map/all_gather | solution.py:47
  36.5 20.4 %all-to-all-start.1 = ((bf16[8,128,256]{2,1,0:T(8,128)(2,1)}), bf16[8,128,256]{2,1,0:T(8,128)(2,1)S(1)}, u32[]{:S(2)}, u32[]{:S(2)}) async-start(bf16[8,128,256]{2,1,0:T(8,128)(2,1)} %gather_fusion), calls=%async_computation.1 | async-start | bytes 1048576 | tf_op jit(solution)/shard_map/all_to_all | solution.py:49
  42.0 48.0 %all-gather.7.cloned.1.call-start = ((), (), s32[]{:S(2)}) async-start(), calls=%async_computation.6 | async-start | bytes 1966080 | tf_op jit(solution)/shard_map/all_gather | solution.py:47
  66.9 3.3 %copy-start.1 = (f32[768,256]{1,0:T(8,128)S(1)}, f32[768,256]{1,0:T(8,128)}, u32[]{:S(2)}) copy-start(f32[768,256]{1,0:T(8,128)} %param.7) | copy-start | bytes 2359300
  66.9 3.3 %copy-start.2 = (s32[768]{0:T(1024)S(1)}, s32[768]{0:T(1024)}, u32[]{:S(2)}) copy-start(s32[768]{0:T(1024)} %param.8) | copy-start | bytes 9220
  72.1 74.1 %all-gather.9.cloned.1.call-start = ((), (), s32[]{:S(2)}) async-start(), calls=%async_computation.7 | async-start | bytes 1966080 | tf_op jit(solution)/shard_map/all_gather | solution.py:47
  128.3 74.1 %all-gather.11.cloned.1.call-start = ((), (), s32[]{:S(2)}) async-start(), calls=%async_computation.8 | async-start | bytes 1966080 | tf_op jit(solution)/shard_map/all_gather | solution.py:47
Sparse Core Ops, SparseCore 0:
  11.3 22.3 all-gather.4
  72.2 17.7 all-gather.6
  128.4 17.7 all-gather.8
  184.6 17.7 all-gather.10
where the time goes:
time: 248 us; the launch traced here: 247 us
  waiting for transfers between devices  76.7 us (31%)
  blocking collectives  74.8 us (30%)
  local copies, waits for them, and re-layouts  39.6 us (16%)
  other arithmetic  24.2 us (10%)
  between operations  13.3 us (5%)
  matrix products  13 us (5%)
  starting transfers between devices  5.64 us (2%)
    all_gather x4, waiting for transfers between devices, local(): group_blocks = lax.all_gather(sent_blocks, 'cols', axis=0, tiled=True)  61.9 us
    all_to_all x3, blocking collectives, local(): lax.all_to_all(reply, 'rows', split_axis=0, concat_axis=0, tiled=True)  61.2 us
    gather x4, local copies, waits for them, and re-layouts, local(): table[table_index].reshape(blocks_dev, degree, block_rows, classes)  28.2 us
    all_to_all x1, waiting for transfers between devices, local(): lax.all_to_all(reply, 'rows', split_axis=0, concat_axis=0, tiled=True)  14.7 us
    all_to_all x1, blocking collectives, ask_blocks(): lax.all_to_all(wanted.reshape(n_rows, 1), 'rows', split_axis=0, concat_ax...  13.6 us
    dot_general x4, matrix products, local(): jnp.einsum('bkij,bkjc->bic', adjacency_tiles, operand, preferred_element_...  13 us
    concatenate x4, other arithmetic, local(): table = jnp.concatenate([group_blocks, remote], axis=0)  11.8 us
    gather x4, local copies, waits for them, and re-layouts, local(): reply = group_blocks[asked[:, 0]]  11.1 us
  transfers between devices with their start and end apart: 5, of which 5 were waited for; matrix products, arithmetic and copies ran while one was open for 0% of the time, Pallas kernels for 0%

commit v1 on v0

--- a/solution.py
+++ b/solution.py
@@ -46,7 +46,19 @@
         sent_blocks = labels.astype(jnp.bfloat16).reshape(blocks_dev, block_rows, classes)
         group_blocks = lax.all_gather(sent_blocks, "cols", axis=0, tiled=True)
         reply = group_blocks[asked[:, 0]]
-        remote = lax.all_to_all(reply, "rows", split_axis=0, concat_axis=0, tiled=True)
+        ways, here = (lax.axis_size("rows"), lax.axis_index("rows"))
+        width = reply.shape[0] // ways
+        lengths = list(reply.shape)
+        lengths[0] = width
+        height = lengths[0]
+        lengths[0] = height * ways
+        full = jnp.zeros(lengths, reply.dtype)
+        for mask in range(ways):
+            part = lax.dynamic_slice_in_dim(reply, (here ^ mask) * width, width, axis=0)
+            if mask:
+                part = lax.ppermute(part, "rows", [(d, d ^ mask) for d in range(ways)])
+            full = lax.dynamic_update_slice_in_dim(full, part, (here ^ mask) * height, axis=0)
+        remote = full
         table = jnp.concatenate([group_blocks, remote], axis=0)
         operand = table[table_index].reshape(blocks_dev, degree, block_rows, classes)
         spread = jnp.einsum(

time: 248 us -> 238 us (0.960)
  blocking collectives: 74.8 us -> 0 us
  starting transfers between devices: 5.64 us -> 52.7 us
  waiting for transfers between devices: 76.7 us -> 95.5 us
  other arithmetic: 24.2 us -> 18.5 us
  local copies, waits for them, and re-layouts: 39.6 us -> 43.6 us
    all_to_all x4 -> x0, blocking collectives: 74.8 us -> none  [the longest x3 61.2 us: local(): lax.all_to_all(reply, 'rows', split_axis=0, concat_axis=0, tiled=True)]
    ppermute x0 -> x28, starting transfers between devices: none -> 45.1 us  [local(): part = lax.ppermute(part, 'rows', [(d, d ^ mask) for d in range(ways)])]
    ppermute x0 -> x28, waiting for transfers between devices: none -> 25.9 us  [local(): part = lax.ppermute(part, 'rows', [(d, d ^ mask) for d in range(ways)])]
    all_to_all x1, waiting for transfers between devices: 14.7 us -> 6.33 us  [ask_blocks(): lax.all_to_all(wanted.reshape(n_rows, 1), 'rows', split_axis=0, concat_ax...]
    concatenate x4, other arithmetic: 11.8 us -> 6.18 us  [local(): table = jnp.concatenate([group_blocks, remote], axis=0)]
    dynamic_slice x0 -> x4, local copies, waits for them, and re-layouts: none -> 3.72 us  [local(): part = lax.dynamic_slice_in_dim(reply, (here ^ mask) * width, width, axis=0)]
  transfers between devices with their start and end apart: 5 -> 33, of which waited for: 5 -> 13; matrix products, arithmetic and copies ran while one was open for 0% -> 1% of each run, Pallas kernels for 0% -> 0%
where the time goes in v1:
time: 238 us; the launch traced here: 237 us
  waiting for transfers between devices  95.5 us (40%)
  starting transfers between devices  52.7 us (22%)
  local copies, waits for them, and re-layouts  43.6 us (18%)
  other arithmetic  18.5 us (8%)
  between operations  13.7 us (6%)
  matrix products  13.1 us (6%)
    all_gather x4, waiting for transfers between devices, local(): group_blocks = lax.all_gather(sent_blocks, 'cols', axis=0, tiled=True)  63.2 us
    ppermute x28, starting transfers between devices, local(): part = lax.ppermute(part, 'rows', [(d, d ^ mask) for d in range(ways)])  45.1 us
    gather x4, local copies, waits for them, and re-layouts, local(): table[table_index].reshape(blocks_dev, degree, block_rows, classes)  28.3 us
    ppermute x28, waiting for transfers between devices, local(): part = lax.ppermute(part, 'rows', [(d, d ^ mask) for d in range(ways)])  25.9 us
    dot_general x4, matrix products, local(): jnp.einsum('bkij,bkjc->bic', adjacency_tiles, operand, preferred_element_...  13.1 us
    gather x4, local copies, waits for them, and re-layouts, local(): reply = group_blocks[asked[:, 0]]  10.3 us
    all_to_all x1, starting transfers between devices, ask_blocks(): lax.all_to_all(wanted.reshape(n_rows, 1), 'rows', split_axis=0, concat_ax...  7.31 us
    all_to_all x1, waiting for transfers between devices, ask_blocks(): lax.all_to_all(wanted.reshape(n_rows, 1), 'rows', split_axis=0, concat_ax...  6.33 us
  transfers between devices with their start and end apart: 33, of which 13 were waited for; matrix products, arithmetic and copies ran while one was open for 1% of the time, Pallas kernels for 0%

profile of v1, /device:TPU:0, one launch (start us, length us, event | category | flops | bytes accessed | tf_op | source)
XLA Modules:
  0.0 237.0 jit_solution(4067101596776896205)
XLA Ops:
  7.4 1.5 fusion.11
  8.9 2.3 multiply_convert_fusion.3
  12.2 7.3 %all-to-all-start = ((s32[8,1,1]{2,1,0:T(1,128)}), s32[8,1,1]{2,1,0:T(1,128)S(1)}, u32[]{:S(2)}, u32[]{:S(2)}) async-start(s32[8,1,1]{2,1,0:T(1,128)} %copy.8), calls=%async_computation | async-start | bytes 8192 | tf_op jit(solution)/shard_map/all_to_all | solution.py:25
  19.7 6.3 %all-to-all-done = s32[8,1,1]{2,1,0:T(1,128)S(1)} async-done(((s32[8,1,1]{2,1,0:T(1,128)}), s32[8,1,1]{2,1,0:T(1,128)S(1)}, u32[]{:S(2)}, u32[]{:S(2)}) %all-to-all-start) | async-done | bytes 64 | tf_op jit(solution)/shard_map/all_to_all | solution.py:25
  26.3 7.5 %all-gather.5.cloned.1.call-done = bf16[24,128,256]{2,1,0:T(8,128)(2,1)} async-done(((bf16[6,128,256]{2,1,0:T(8,128)(2,1)}), bf16[24,128,256]{2,1,0:T(8,128)(2,1)}) %all-gather.5.cloned.1.call-update) | async-done | bytes 1572880 | tf_op jit(solution)/shard_map/all_gather | solution.py:47
  33.7 2.0 gather_fusion
  35.8 1.6 collective-permute-start
  37.4 1.5 collective-permute-start.1
  39.4 2.4 %collective-permute-start.3 = (bf16[1,128,256]{2,1,0:T(8,128)(2,1)S(1)}, bf16[1,128,256]{2,1,0:T(8,128)(2,1)S(1)}, u32[]{:S(2)}, u32[]{:S(2)}) collective-permute-start(bf16[1,128,256]{2,1,0:T(8,128)(2,1)S(1)} %get-tuple-element.32), channel_id=1, source_target_pairs={{0,16},{4,20},{8,24},{12,28},{16,0},{20,4},{24,8},{28,12},{1,17},{... | collective-permute-start | bytes 196616 | tf_op jit(solution)/shard_map/ppermute | solution.py:59
  41.8 1.5 collective-permute-start.4
  43.3 3.3 %collective-permute-start.5 = (bf16[1,128,256]{2,1,0:T(8,128)(2,1)S(1)}, bf16[1,128,256]{2,1,0:T(8,128)(2,1)S(1)}, u32[]{:S(2)}, u32[]{:S(2)}) collective-permute-start(bf16[1,128,256]{2,1,0:T(8,128)(2,1)S(1)} %get-tuple-element.30), channel_id=1, source_target_pairs={{0,24},{4,28},{8,16},{12,20},{16,8},{20,12},{24,0},{28,4},{1,25},{... | collective-permute-start | bytes 196616 | tf_op jit(solution)/shard_map/ppermute | solution.py:59
  47.2 5.0 %collective-permute-done.4 = bf16[1,128,256]{2,1,0:T(8,128)(2,1)S(1)} collective-permute-done((bf16[1,128,256]{2,1,0:T(8,128)(2,1)S(1)}, bf16[1,128,256]{2,1,0:T(8,128)(2,1)S(1)}, u32[]{:S(2)}, u32[]{:S(2)}) %collective-permute-start.4) | collective-permute-done | bytes 65568 | tf_op jit(solution)/shard_map/ppermute | solution.py:59
  52.3 1.4 collective-permute-done.6
  53.7 1.5 pad_maximum_fusion
  55.3 7.1 %gather_fusion.1 = bf16[72,128,256]{2,1,0:T(8,128)(2,1)} fusion(bf16[32,128,256]{2,1,0:T(8,128)(2,1)} %pad_maximum_fusion, s32[1024]{0:T(1024)S(1)} %pad_clamp_fusion), kind=kCustom, calls=%fused_computation.1 | custom fusion | bytes 9437472 | tf_op jit(solution)/shard_map/gather | solution.py:63
  62.4 3.3 %fusion = f32[6,256,128]{1,2,0:T(8,128)S(1)} fusion(bf16[6,12,128,128]{3,2,1,0:T(8,128)(2,1)S(1)} %copy-done, bf16[6,12,128,256]{3,2,1,0:T(8,128)(2,1)} %bitcast.77), kind=kOutput, calls=%fused_computation.16 | convolution fusion | flops 604176384 | bytes 7864320 | tf_op jit(solution)/shard_map/bkij,bkjc->bic/dot_general | solution.py:64
  67.6 18.6 %all-gather.7.cloned.1.call-done = bf16[24,128,256]{2,1,0:T(8,128)(2,1)} async-done(((bf16[6,128,256]{2,1,0:T(8,128)(2,1)}), bf16[24,128,256]{2,1,0:T(8,128)(2,1)}) %all-gather.7.cloned.1.call-update) | async-done | bytes 1572880 | tf_op jit(solution)/shard_map/all_gather | solution.py:47
  86.2 2.8 %gather_fusion.2 = bf16[8,128,256]{2,1,0:T(8,128)(2,1)} fusion(bf16[24,128,256]{2,1,0:T(8,128)(2,1)} %all-gather.7.cloned.1.call-done, s32[1024]{0:T(1024)S(1)} %pad_clamp_fusion.1), kind=kCustom, calls=%fused_computation.2 | custom fusion | bytes 1048608 | tf_op jit(solution)/shard_map/gather | solution.py:48
  90.2 1.5 collective-permute-start.7
  91.8 1.5 collective-permute-start.8
  93.8 2.4 %collective-permute-start.10 = (bf16[1,128,256]{2,1,0:T(8,128)(2,1)S(1)}, bf16[1,128,256]{2,1,0:T(8,128)(2,1)S(1)}, u32[]{:S(2)}, u32[]{:S(2)}) collective-permute-start(bf16[1,128,256]{2,1,0:T(8,128)(2,1)S(1)} %get-tuple-element.24), channel_id=1, source_target_pairs={{0,16},{4,20},{8,24},{12,28},{16,0},{20,4},{24,8},{28,12},{1,17},{... | collective-permute-start | bytes 196616 | tf_op jit(solution)/shard_map/ppermute | solution.py:59
  97.6 3.3 %collective-permute-start.12 = (bf16[1,128,256]{2,1,0:T(8,128)(2,1)S(1)}, bf16[1,128,256]{2,1,0:T(8,128)(2,1)S(1)}, u32[]{:S(2)}, u32[]{:S(2)}) collective-permute-start(bf16[1,128,256]{2,1,0:T(8,128)(2,1)S(1)} %get-tuple-element.22), channel_id=1, source_target_pairs={{0,24},{4,28},{8,16},{12,20},{16,8},{20,12},{24,0},{28,4},{1,25},{... | collective-permute-start | bytes 196616 | tf_op jit(solution)/shard_map/ppermute | solution.py:59
  101.6 5.0 %collective-permute-done.11 = bf16[1,128,256]{2,1,0:T(8,128)(2,1)S(1)} collective-permute-done((bf16[1,128,256]{2,1,0:T(8,128)(2,1)S(1)}, bf16[1,128,256]{2,1,0:T(8,128)(2,1)S(1)}, u32[]{:S(2)}, u32[]{:S(2)}) %collective-permute-start.11) | collective-permute-done | bytes 65568 | tf_op jit(solution)/shard_map/ppermute | solution.py:59
  106.7 1.4 collective-permute-done.13
  108.1 1.5 pad_maximum_fusion.1
  109.7 7.1 %gather_fusion.3 = bf16[72,128,256]{2,1,0:T(8,128)(2,1)} fusion(bf16[32,128,256]{2,1,0:T(8,128)(2,1)} %pad_maximum_fusion.1, s32[1024]{0:T(1024)S(1)} %pad_clamp_fusion), kind=kCustom, calls=%fused_computation.3 | custom fusion | bytes 9437472 | tf_op jit(solution)/shard_map/gather | solution.py:63
  116.7 3.2 %fusion.1 = f32[6,256,128]{1,2,0:T(8,128)S(1)} fusion(bf16[6,12,128,128]{3,2,1,0:T(8,128)(2,1)S(1)} %copy-done, bf16[6,12,128,256]{3,2,1,0:T(8,128)(2,1)} %bitcast.78), kind=kOutput, calls=%fused_computation.17 | convolution fusion | flops 604176384 | bytes 7864320 | tf_op jit(solution)/shard_map/bkij,bkjc->bic/dot_general | solution.py:64
  122.1 18.4 %all-gather.9.cloned.1.call-done = bf16[24,128,256]{2,1,0:T(8,128)(2,1)} async-done(((bf16[6,128,256]{2,1,0:T(8,128)(2,1)}), bf16[24,128,256]{2,1,0:T(8,128)(2,1)}) %all-gather.9.cloned.1.call-update) | async-done | bytes 1572880 | tf_op jit(solution)/shard_map/all_gather | solution.py:47
  140.5 2.8 %gather_fusion.4 = bf16[8,128,256]{2,1,0:T(8,128)(2,1)} fusion(bf16[24,128,256]{2,1,0:T(8,128)(2,1)} %all-gather.9.cloned.1.call-done, s32[1024]{0:T(1024)S(1)} %pad_clamp_fusion.1), kind=kCustom, calls=%fused_computation.4 | custom fusion | bytes 1048608 | tf_op jit(solution)/shard_map/gather | solution.py:48
  144.5 1.5 collective-permute-start.14
  146.1 1.5 collective-permute-start.15
  148.1 2.4 %collective-permute-start.17 = (bf16[1,128,256]{2,1,0:T(8,128)(2,1)S(1)}, bf16[1,128,256]{2,1,0:T(8,128)(2,1)S(1)}, u32[]{:S(2)}, u32[]{:S(2)}) collective-permute-start(bf16[1,128,256]{2,1,0:T(8,128)(2,1)S(1)} %get-tuple-element.16), channel_id=1, source_target_pairs={{0,16},{4,20},{8,24},{12,28},{16,0},{20,4},{24,8},{28,12},{1,17},{... | collective-permute-start | bytes 196616 | tf_op jit(solution)/shard_map/ppermute | solution.py:59
  151.9 3.3 %collective-permute-start.19 = (bf16[1,128,256]{2,1,0:T(8,128)(2,1)S(1)}, bf16[1,128,256]{2,1,0:T(8,128)(2,1)S(1)}, u32[]{:S(2)}, u32[]{:S(2)}) collective-permute-start(bf16[1,128,256]{2,1,0:T(8,128)(2,1)S(1)} %get-tuple-element.14), channel_id=1, source_target_pairs={{0,24},{4,28},{8,16},{12,20},{16,8},{20,12},{24,0},{28,4},{1,25},{... | collective-permute-start | bytes 196616 | tf_op jit(solution)/shard_map/ppermute | solution.py:59
  155.9 5.0 %collective-permute-done.18 = bf16[1,128,256]{2,1,0:T(8,128)(2,1)S(1)} collective-permute-done((bf16[1,128,256]{2,1,0:T(8,128)(2,1)S(1)}, bf16[1,128,256]{2,1,0:T(8,128)(2,1)S(1)}, u32[]{:S(2)}, u32[]{:S(2)}) %collective-permute-start.18) | collective-permute-done | bytes 65568 | tf_op jit(solution)/shard_map/ppermute | solution.py:59
  161.0 1.4 collective-permute-done.20
  162.4 1.5 pad_maximum_fusion.2
  164.0 7.1 %gather_fusion.5 = bf16[72,128,256]{2,1,0:T(8,128)(2,1)} fusion(bf16[32,128,256]{2,1,0:T(8,128)(2,1)} %pad_maximum_fusion.2, s32[1024]{0:T(1024)S(1)} %pad_clamp_fusion), kind=kCustom, calls=%fused_computation.5 | custom fusion | bytes 9437472 | tf_op jit(solution)/shard_map/gather | solution.py:63
  171.0 3.2 %fusion.2 = f32[6,256,128]{1,2,0:T(8,128)S(1)} fusion(bf16[6,12,128,128]{3,2,1,0:T(8,128)(2,1)S(1)} %copy-done, bf16[6,12,128,256]{3,2,1,0:T(8,128)(2,1)} %bitcast.79), kind=kOutput, calls=%fused_computation.18 | convolution fusion | flops 604176384 | bytes 7864320 | tf_op jit(solution)/shard_map/bkij,bkjc->bic/dot_general | solution.py:64
  176.1 18.7 %all-gather.11.cloned.1.call-done = bf16[24,128,256]{2,1,0:T(8,128)(2,1)} async-done(((bf16[6,128,256]{2,1,0:T(8,128)(2,1)}), bf16[24,128,256]{2,1,0:T(8,128)(2,1)}) %all-gather.11.cloned.1.call-update) | async-done | bytes 1572880 | tf_op jit(solution)/shard_map/all_gather | solution.py:47
  194.8 2.8 %gather_fusion.6 = bf16[8,128,256]{2,1,0:T(8,128)(2,1)} fusion(bf16[24,128,256]{2,1,0:T(8,128)(2,1)} %all-gather.11.cloned.1.call-done, s32[1024]{0:T(1024)S(1)} %pad_clamp_fusion.1), kind=kCustom, calls=%fused_computation.6 | custom fusion | bytes 1048608 | tf_op jit(solution)/shard_map/gather | solution.py:48
  198.8 1.5 collective-permute-start.21
  200.4 1.5 collective-permute-start.22
  202.4 2.4 %collective-permute-start.24 = (bf16[1,128,256]{2,1,0:T(8,128)(2,1)S(1)}, bf16[1,128,256]{2,1,0:T(8,128)(2,1)S(1)}, u32[]{:S(2)}, u32[]{:S(2)}) collective-permute-start(bf16[1,128,256]{2,1,0:T(8,128)(2,1)S(1)} %get-tuple-element.8), channel_id=1, source_target_pairs={{0,16},{4,20},{8,24},{12,28},{16,0},{20,4},{24,8},{28,12},{1,17},{... | collective-permute-start | bytes 196616 | tf_op jit(solution)/shard_map/ppermute | solution.py:59
  206.2 3.3 %collective-permute-start.26 = (bf16[1,128,256]{2,1,0:T(8,128)(2,1)S(1)}, bf16[1,128,256]{2,1,0:T(8,128)(2,1)S(1)}, u32[]{:S(2)}, u32[]{:S(2)}) collective-permute-start(bf16[1,128,256]{2,1,0:T(8,128)(2,1)S(1)} %get-tuple-element.6), channel_id=1, source_target_pairs={{0,24},{4,28},{8,16},{12,20},{16,8},{20,12},{24,0},{28,4},{1,25},{... | collective-permute-start | bytes 196616 | tf_op jit(solution)/shard_map/ppermute | solution.py:59
  210.2 5.0 %collective-permute-done.25 = bf16[1,128,256]{2,1,0:T(8,128)(2,1)S(1)} collective-permute-done((bf16[1,128,256]{2,1,0:T(8,128)(2,1)S(1)}, bf16[1,128,256]{2,1,0:T(8,128)(2,1)S(1)}, u32[]{:S(2)}, u32[]{:S(2)}) %collective-permute-start.25) | collective-permute-done | bytes 65568 | tf_op jit(solution)/shard_map/ppermute | solution.py:59
  216.7 1.5 pad_maximum_fusion.3
  218.3 7.1 %gather_fusion.7 = bf16[72,128,256]{2,1,0:T(8,128)(2,1)} fusion(bf16[32,128,256]{2,1,0:T(8,128)(2,1)} %pad_maximum_fusion.3, s32[1024]{0:T(1024)S(1)} %pad_clamp_fusion), kind=kCustom, calls=%fused_computation.7 | custom fusion | bytes 9437472 | tf_op jit(solution)/shard_map/gather | solution.py:63
  225.3 3.2 %fusion.3 = f32[6,256,128]{1,2,0:T(8,128)S(1)} fusion(bf16[6,12,128,128]{3,2,1,0:T(8,128)(2,1)S(1)} %copy-done, bf16[6,12,128,256]{3,2,1,0:T(8,128)(2,1)} %bitcast.76), kind=kOutput, calls=%fused_computation.19 | convolution fusion | flops 604176384 | bytes 7864320 | tf_op jit(solution)/shard_map/bkij,bkjc->bic/dot_general | solution.py:64
  (118 shorter events, 24.0 us)
Async XLA Ops:
  6.5 55.8 %copy-start = (bf16[6,12,128,128]{3,2,1,0:T(8,128)(2,1)S(1)}, bf16[6,12,128,128]{3,2,1,0:T(8,128)(2,1)}, u32[]{:S(2)}) copy-start(bf16[6,12,128,128]{3,2,1,0:T(8,128)(2,1)} %param.5) | copy-start | bytes 7077892
  6.5 4.7 %copy-start.7 = (s32[6,12]{1,0:T(8,128)S(1)}, s32[6,12]{1,0:T(8,128)}, u32[]{:S(2)}) copy-start(s32[6,12]{1,0:T(8,128)} %param.6) | copy-start | bytes 868
  6.5 27.2 %all-gather.5.cloned.1.call-start = ((), (), s32[]{:S(2)}) async-start(), calls=%async_computation.1 | async-start | bytes 1966080 | tf_op jit(solution)/shard_map/all_gather | solution.py:47
  12.2 13.8 %all-to-all-start = ((s32[8,1,1]{2,1,0:T(1,128)}), s32[8,1,1]{2,1,0:T(1,128)S(1)}, u32[]{:S(2)}, u32[]{:S(2)}) async-start(s32[8,1,1]{2,1,0:T(1,128)} %copy.8), calls=%async_computation | async-start | bytes 8192 | tf_op jit(solution)/shard_map/all_to_all | solution.py:25
  19.5 66.7 %all-gather.7.cloned.1.call-start = ((), (), s32[]{:S(2)}) async-start(), calls=%async_computation.2 | async-start | bytes 1966080 | tf_op jit(solution)/shard_map/all_gather | solution.py:47
  35.7 18.0 %copy-start.2 = (bf16[24,128,256]{2,1,0:T(8,128)(2,1)S(1)}, bf16[24,128,256]{2,1,0:T(8,128)(2,1)}, u32[]{:S(2)}) copy-start(bf16[24,128,256]{2,1,0:T(8,128)(2,1)} %all-gather.5.cloned.1.call-done) | copy-start | bytes 4718596
  35.8 7.4 %collective-permute-start = (bf16[1,128,256]{2,1,0:T(8,128)(2,1)S(1)}, bf16[1,128,256]{2,1,0:T(8,128)(2,1)S(1)}, u32[]{:S(2)}, u32[]{:S(2)}) collective-permute-start(bf16[1,128,256]{2,1,0:T(8,128)(2,1)S(1)} %get-tuple-element.35), channel_id=1, source_target_pairs={{0,4},{4,0},{8,12},{12,8},{16,20},{20,16},{24,28},{28,24},{1,5},{5... | collective-permute-start | bytes 196616 | tf_op jit(solution)/shard_map/ppermute | solution.py:59
  37.4 9.2 %collective-permute-start.1 = (bf16[1,128,256]{2,1,0:T(8,128)(2,1)S(1)}, bf16[1,128,256]{2,1,0:T(8,128)(2,1)S(1)}, u32[]{:S(2)}, u32[]{:S(2)}) collective-permute-start(bf16[1,128,256]{2,1,0:T(8,128)(2,1)S(1)} %get-tuple-element.34), channel_id=1, source_target_pairs={{0,8},{4,12},{8,0},{12,4},{16,24},{20,28},{24,16},{28,20},{1,9},{5... | collective-permute-start | bytes 196616 | tf_op jit(solution)/shard_map/ppermute | solution.py:59
  38.9 8.3 %collective-permute-start.2 = (bf16[1,128,256]{2,1,0:T(8,128)(2,1)S(1)}, bf16[1,128,256]{2,1,0:T(8,128)(2,1)S(1)}, u32[]{:S(2)}, u32[]{:S(2)}) collective-permute-start(bf16[1,128,256]{2,1,0:T(8,128)(2,1)S(1)} %get-tuple-element.33), channel_id=1, source_target_pairs={{0,12},{4,8},{8,4},{12,0},{16,28},{20,24},{24,20},{28,16},{1,13},{... | collective-permute-start | bytes 196616 | tf_op jit(solution)/shard_map/ppermute | solution.py:59
  39.4 7.8 %collective-permute-start.3 = (bf16[1,128,256]{2,1,0:T(8,128)(2,1)S(1)}, bf16[1,128,256]{2,1,0:T(8,128)(2,1)S(1)}, u32[]{:S(2)}, u32[]{:S(2)}) collective-permute-start(bf16[1,128,256]{2,1,0:T(8,128)(2,1)S(1)} %get-tuple-element.32), channel_id=1, source_target_pairs={{0,16},{4,20},{8,24},{12,28},{16,0},{20,4},{24,8},{28,12},{1,17},{... | collective-permute-start | bytes 196616 | tf_op jit(solution)/shard_map/ppermute | solution.py:59
  41.8 10.4 %collective-permute-start.4 = (bf16[1,128,256]{2,1,0:T(8,128)(2,1)S(1)}, bf16[1,128,256]{2,1,0:T(8,128)(2,1)S(1)}, u32[]{:S(2)}, u32[]{:S(2)}) collective-permute-start(bf16[1,128,256]{2,1,0:T(8,128)(2,1)S(1)} %get-tuple-element.31), channel_id=1, source_target_pairs={{0,20},{4,16},{8,28},{12,24},{16,4},{20,0},{24,12},{28,8},{1,21},{... | collective-permute-start | bytes 196616 | tf_op jit(solution)/shard_map/ppermute | solution.py:59
  43.3 9.0 %collective-permute-start.5 = (bf16[1,128,256]{2,1,0:T(8,128)(2,1)S(1)}, bf16[1,128,256]{2,1,0:T(8,128)(2,1)S(1)}, u32[]{:S(2)}, u32[]{:S(2)}) collective-permute-start(bf16[1,128,256]{2,1,0:T(8,128)(2,1)S(1)} %get-tuple-element.30), channel_id=1, source_target_pairs={{0,24},{4,28},{8,16},{12,20},{16,8},{20,12},{24,0},{28,4},{1,25},{... | collective-permute-start | bytes 196616 | tf_op jit(solution)/shard_map/ppermute | solution.py:59
  46.6 7.1 %collective-permute-start.6 = (bf16[1,128,256]{2,1,0:T(8,128)(2,1)S(1)}, bf16[1,128,256]{2,1,0:T(8,128)(2,1)S(1)}, u32[]{:S(2)}, u32[]{:S(2)}) collective-permute-start(bf16[1,128,256]{2,1,0:T(8,128)(2,1)S(1)} %get-tuple-element.29), channel_id=1, source_target_pairs={{0,28},{4,24},{8,20},{12,16},{16,12},{20,8},{24,4},{28,0},{1,29},{... | collective-permute-start | bytes 196616 | tf_op jit(solution)/shard_map/ppermute | solution.py:59
  62.4 3.3 %copy-start.1 = (f32[768,256]{1,0:T(8,128)S(1)}, f32[768,256]{1,0:T(8,128)}, u32[]{:S(2)}) copy-start(f32[768,256]{1,0:T(8,128)} %param.7) | copy-start | bytes 2359300
  62.4 3.3 %copy-start.6 = (s32[768]{0:T(1024)S(1)}, s32[768]{0:T(1024)}, u32[]{:S(2)}) copy-start(s32[768]{0:T(1024)} %param.8) | copy-start | bytes 9220
  67.5 73.0 %all-gather.9.cloned.1.call-start = ((), (), s32[]{:S(2)}) async-start(), calls=%async_computation.3 | async-start | bytes 1966080 | tf_op jit(solution)/shard_map/all_gather | solution.py:47
  89.0 19.2 %copy-start.4 = (bf16[24,128,256]{2,1,0:T(8,128)(2,1)S(1)}, bf16[24,128,256]{2,1,0:T(8,128)(2,1)}, u32[]{:S(2)}) copy-start(bf16[24,128,256]{2,1,0:T(8,128)(2,1)} %all-gather.7.cloned.1.call-done) | copy-start | bytes 4718596
  90.2 7.4 %collective-permute-start.7 = (bf16[1,128,256]{2,1,0:T(8,128)(2,1)S(1)}, bf16[1,128,256]{2,1,0:T(8,128)(2,1)S(1)}, u32[]{:S(2)}, u32[]{:S(2)}) collective-permute-start(bf16[1,128,256]{2,1,0:T(8,128)(2,1)S(1)} %get-tuple-element.27), channel_id=1, source_target_pairs={{0,4},{4,0},{8,12},{12,8},{16,20},{20,16},{24,28},{28,24},{1,5},{5... | collective-permute-start | bytes 196616 | tf_op jit(solution)/shard_map/ppermute | solution.py:59
  91.8 9.2 %collective-permute-start.8 = (bf16[1,128,256]{2,1,0:T(8,128)(2,1)S(1)}, bf16[1,128,256]{2,1,0:T(8,128)(2,1)S(1)}, u32[]{:S(2)}, u32[]{:S(2)}) collective-permute-start(bf16[1,128,256]{2,1,0:T(8,128)(2,1)S(1)} %get-tuple-element.26), channel_id=1, source_target_pairs={{0,8},{4,12},{8,0},{12,4},{16,24},{20,28},{24,16},{28,20},{1,9},{5... | collective-permute-start | bytes 196616 | tf_op jit(solution)/shard_map/ppermute | solution.py:59
  93.3 8.3 %collective-permute-start.9 = (bf16[1,128,256]{2,1,0:T(8,128)(2,1)S(1)}, bf16[1,128,256]{2,1,0:T(8,128)(2,1)S(1)}, u32[]{:S(2)}, u32[]{:S(2)}) collective-permute-start(bf16[1,128,256]{2,1,0:T(8,128)(2,1)S(1)} %get-tuple-element.25), channel_id=1, source_target_pairs={{0,12},{4,8},{8,4},{12,0},{16,28},{20,24},{24,20},{28,16},{1,13},{... | collective-permute-start | bytes 196616 | tf_op jit(solution)/shard_map/ppermute | solution.py:59
  93.8 7.8 %collective-permute-start.10 = (bf16[1,128,256]{2,1,0:T(8,128)(2,1)S(1)}, bf16[1,128,256]{2,1,0:T(8,128)(2,1)S(1)}, u32[]{:S(2)}, u32[]{:S(2)}) collective-permute-start(bf16[1,128,256]{2,1,0:T(8,128)(2,1)S(1)} %get-tuple-element.24), channel_id=1, source_target_pairs={{0,16},{4,20},{8,24},{12,28},{16,0},{20,4},{24,8},{28,12},{1,17},{... | collective-permute-start | bytes 196616 | tf_op jit(solution)/shard_map/ppermute | solution.py:59
  96.2 10.4 %collective-permute-start.11 = (bf16[1,128,256]{2,1,0:T(8,128)(2,1)S(1)}, bf16[1,128,256]{2,1,0:T(8,128)(2,1)S(1)}, u32[]{:S(2)}, u32[]{:S(2)}) collective-permute-start(bf16[1,128,256]{2,1,0:T(8,128)(2,1)S(1)} %get-tuple-element.23), channel_id=1, source_target_pairs={{0,20},{4,16},{8,28},{12,24},{16,4},{20,0},{24,12},{28,8},{1,21},{... | collective-permute-start | bytes 196616 | tf_op jit(solution)/shard_map/ppermute | solution.py:59
  97.6 9.0 %collective-permute-start.12 = (bf16[1,128,256]{2,1,0:T(8,128)(2,1)S(1)}, bf16[1,128,256]{2,1,0:T(8,128)(2,1)S(1)}, u32[]{:S(2)}, u32[]{:S(2)}) collective-permute-start(bf16[1,128,256]{2,1,0:T(8,128)(2,1)S(1)} %get-tuple-element.22), channel_id=1, source_target_pairs={{0,24},{4,28},{8,16},{12,20},{16,8},{20,12},{24,0},{28,4},{1,25},{... | collective-permute-start | bytes 196616 | tf_op jit(solution)/shard_map/ppermute | solution.py:59
  101.0 7.1 %collective-permute-start.13 = (bf16[1,128,256]{2,1,0:T(8,128)(2,1)S(1)}, bf16[1,128,256]{2,1,0:T(8,128)(2,1)S(1)}, u32[]{:S(2)}, u32[]{:S(2)}) collective-permute-start(bf16[1,128,256]{2,1,0:T(8,128)(2,1)S(1)} %get-tuple-element.21), channel_id=1, source_target_pairs={{0,28},{4,24},{8,20},{12,16},{16,12},{20,8},{24,4},{28,0},{1,29},{... | collective-permute-start | bytes 196616 | tf_op jit(solution)/shard_map/ppermute | solution.py:59
  121.8 72.9 %all-gather.11.cloned.1.call-start = ((), (), s32[]{:S(2)}) async-start(), calls=%async_computation.4 | async-start | bytes 1966080 | tf_op jit(solution)/shard_map/all_gather | solution.py:47
  143.3 19.2 %copy-start.5 = (bf16[24,128,256]{2,1,0:T(8,128)(2,1)S(1)}, bf16[24,128,256]{2,1,0:T(8,128)(2,1)}, u32[]{:S(2)}) copy-start(bf16[24,128,256]{2,1,0:T(8,128)(2,1)} %all-gather.9.cloned.1.call-done) | copy-start | bytes 4718596
  144.5 7.4 %collective-permute-start.14 = (bf16[1,128,256]{2,1,0:T(8,128)(2,1)S(1)}, bf16[1,128,256]{2,1,0:T(8,128)(2,1)S(1)}, u32[]{:S(2)}, u32[]{:S(2)}) collective-permute-start(bf16[1,128,256]{2,1,0:T(8,128)(2,1)S(1)} %get-tuple-element.19), channel_id=1, source_target_pairs={{0,4},{4,0},{8,12},{12,8},{16,20},{20,16},{24,28},{28,24},{1,5},{5... | collective-permute-start | bytes 196616 | tf_op jit(solution)/shard_map/ppermute | solution.py:59
  146.1 9.2 %collective-permute-start.15 = (bf16[1,128,256]{2,1,0:T(8,128)(2,1)S(1)}, bf16[1,128,256]{2,1,0:T(8,128)(2,1)S(1)}, u32[]{:S(2)}, u32[]{:S(2)}) collective-permute-start(bf16[1,128,256]{2,1,0:T(8,128)(2,1)S(1)} %get-tuple-element.18), channel_id=1, source_target_pairs={{0,8},{4,12},{8,0},{12,4},{16,24},{20,28},{24,16},{28,20},{1,9},{5... | collective-permute-start | bytes 196616 | tf_op jit(solution)/shard_map/ppermute | solution.py:59
  147.6 8.3 %collective-permute-start.16 = (bf16[1,128,256]{2,1,0:T(8,128)(2,1)S(1)}, bf16[1,128,256]{2,1,0:T(8,128)(2,1)S(1)}, u32[]{:S(2)}, u32[]{:S(2)}) collective-permute-start(bf16[1,128,256]{2,1,0:T(8,128)(2,1)S(1)} %get-tuple-element.17), channel_id=1, source_target_pairs={{0,12},{4,8},{8,4},{12,0},{16,28},{20,24},{24,20},{28,16},{1,13},{... | collective-permute-start | bytes 196616 | tf_op jit(solution)/shard_map/ppermute | solution.py:59
  148.1 7.8 %collective-permute-start.17 = (bf16[1,128,256]{2,1,0:T(8,128)(2,1)S(1)}, bf16[1,128,256]{2,1,0:T(8,128)(2,1)S(1)}, u32[]{:S(2)}, u32[]{:S(2)}) collective-permute-start(bf16[1,128,256]{2,1,0:T(8,128)(2,1)S(1)} %get-tuple-element.16), channel_id=1, source_target_pairs={{0,16},{4,20},{8,24},{12,28},{16,0},{20,4},{24,8},{28,12},{1,17},{... | collective-permute-start | bytes 196616 | tf_op jit(solution)/shard_map/ppermute | solution.py:59
  150.5 10.4 %collective-permute-start.18 = (bf16[1,128,256]{2,1,0:T(8,128)(2,1)S(1)}, bf16[1,128,256]{2,1,0:T(8,128)(2,1)S(1)}, u32[]{:S(2)}, u32[]{:S(2)}) collective-permute-start(bf16[1,128,256]{2,1,0:T(8,128)(2,1)S(1)} %get-tuple-element.15), channel_id=1, source_target_pairs={{0,20},{4,16},{8,28},{12,24},{16,4},{20,0},{24,12},{28,8},{1,21},{... | collective-permute-start | bytes 196616 | tf_op jit(solution)/shard_map/ppermute | solution.py:59
  151.9 9.0 %collective-permute-start.19 = (bf16[1,128,256]{2,1,0:T(8,128)(2,1)S(1)}, bf16[1,128,256]{2,1,0:T(8,128)(2,1)S(1)}, u32[]{:S(2)}, u32[]{:S(2)}) collective-permute-start(bf16[1,128,256]{2,1,0:T(8,128)(2,1)S(1)} %get-tuple-element.14), channel_id=1, source_target_pairs={{0,24},{4,28},{8,16},{12,20},{16,8},{20,12},{24,0},{28,4},{1,25},{... | collective-permute-start | bytes 196616 | tf_op jit(solution)/shard_map/ppermute | solution.py:59
  155.3 7.1 %collective-permute-start.20 = (bf16[1,128,256]{2,1,0:T(8,128)(2,1)S(1)}, bf16[1,128,256]{2,1,0:T(8,128)(2,1)S(1)}, u32[]{:S(2)}, u32[]{:S(2)}) collective-permute-start(bf16[1,128,256]{2,1,0:T(8,128)(2,1)S(1)} %get-tuple-element.13), channel_id=1, source_target_pairs={{0,28},{4,24},{8,20},{12,16},{16,12},{20,8},{24,4},{28,0},{1,29},{... | collective-permute-start | bytes 196616 | tf_op jit(solution)/shard_map/ppermute | solution.py:59
  197.6 19.2 %copy-start.3 = (bf16[24,128,256]{2,1,0:T(8,128)(2,1)S(1)}, bf16[24,128,256]{2,1,0:T(8,128)(2,1)}, u32[]{:S(2)}) copy-start(bf16[24,128,256]{2,1,0:T(8,128)(2,1)} %all-gather.11.cloned.1.call-done) | copy-start | bytes 4718596
  198.8 7.4 %collective-permute-start.21 = (bf16[1,128,256]{2,1,0:T(8,128)(2,1)S(1)}, bf16[1,128,256]{2,1,0:T(8,128)(2,1)S(1)}, u32[]{:S(2)}, u32[]{:S(2)}) collective-permute-start(bf16[1,128,256]{2,1,0:T(8,128)(2,1)S(1)} %get-tuple-element.11), channel_id=1, source_target_pairs={{0,4},{4,0},{8,12},{12,8},{16,20},{20,16},{24,28},{28,24},{1,5},{5... | collective-permute-start | bytes 196616 | tf_op jit(solution)/shard_map/ppermute | solution.py:59
  200.4 9.2 %collective-permute-start.22 = (bf16[1,128,256]{2,1,0:T(8,128)(2,1)S(1)}, bf16[1,128,256]{2,1,0:T(8,128)(2,1)S(1)}, u32[]{:S(2)}, u32[]{:S(2)}) collective-permute-start(bf16[1,128,256]{2,1,0:T(8,128)(2,1)S(1)} %get-tuple-element.10), channel_id=1, source_target_pairs={{0,8},{4,12},{8,0},{12,4},{16,24},{20,28},{24,16},{28,20},{1,9},{5... | collective-permute-start | bytes 196616 | tf_op jit(solution)/shard_map/ppermute | solution.py:59
  201.8 8.3 %collective-permute-start.23 = (bf16[1,128,256]{2,1,0:T(8,128)(2,1)S(1)}, bf16[1,128,256]{2,1,0:T(8,128)(2,1)S(1)}, u32[]{:S(2)}, u32[]{:S(2)}) collective-permute-start(bf16[1,128,256]{2,1,0:T(8,128)(2,1)S(1)} %get-tuple-element.9), channel_id=1, source_target_pairs={{0,12},{4,8},{8,4},{12,0},{16,28},{20,24},{24,20},{28,16},{1,13},{... | collective-permute-start | bytes 196616 | tf_op jit(solution)/shard_map/ppermute | solution.py:59
  202.4 7.8 %collective-permute-start.24 = (bf16[1,128,256]{2,1,0:T(8,128)(2,1)S(1)}, bf16[1,128,256]{2,1,0:T(8,128)(2,1)S(1)}, u32[]{:S(2)}, u32[]{:S(2)}) collective-permute-start(bf16[1,128,256]{2,1,0:T(8,128)(2,1)S(1)} %get-tuple-element.8), channel_id=1, source_target_pairs={{0,16},{4,20},{8,24},{12,28},{16,0},{20,4},{24,8},{28,12},{1,17},{... | collective-permute-start | bytes 196616 | tf_op jit(solution)/shard_map/ppermute | solution.py:59
  204.8 10.4 %collective-permute-start.25 = (bf16[1,128,256]{2,1,0:T(8,128)(2,1)S(1)}, bf16[1,128,256]{2,1,0:T(8,128)(2,1)S(1)}, u32[]{:S(2)}, u32[]{:S(2)}) collective-permute-start(bf16[1,128,256]{2,1,0:T(8,128)(2,1)S(1)} %get-tuple-element.7), channel_id=1, source_target_pairs={{0,20},{4,16},{8,28},{12,24},{16,4},{20,0},{24,12},{28,8},{1,21},{... | collective-permute-start | bytes 196616 | tf_op jit(solution)/shard_map/ppermute | solution.py:59
  206.2 9.0 %collective-permute-start.26 = (bf16[1,128,256]{2,1,0:T(8,128)(2,1)S(1)}, bf16[1,128,256]{2,1,0:T(8,128)(2,1)S(1)}, u32[]{:S(2)}, u32[]{:S(2)}) collective-permute-start(bf16[1,128,256]{2,1,0:T(8,128)(2,1)S(1)} %get-tuple-element.6), channel_id=1, source_target_pairs={{0,24},{4,28},{8,16},{12,20},{16,8},{20,12},{24,0},{28,4},{1,25},{... | collective-permute-start | bytes 196616 | tf_op jit(solution)/shard_map/ppermute | solution.py:59
  209.6 7.1 %collective-permute-start.27 = (bf16[1,128,256]{2,1,0:T(8,128)(2,1)S(1)}, bf16[1,128,256]{2,1,0:T(8,128)(2,1)S(1)}, u32[]{:S(2)}, u32[]{:S(2)}) collective-permute-start(bf16[1,128,256]{2,1,0:T(8,128)(2,1)S(1)} %get-tuple-element.5), channel_id=1, source_target_pairs={{0,28},{4,24},{8,20},{12,16},{16,12},{20,8},{24,4},{28,0},{1,29},{... | collective-permute-start | bytes 196616 | tf_op jit(solution)/shard_map/ppermute | solution.py:59
Sparse Core Ops, SparseCore 0:
  11.3 22.3 all-gather.4
  67.7 18.4 all-gather.6
  121.9 18.4 all-gather.8
  176.2 18.4 all-gather.10
